TPU v7x, 32 devices: a 4x4x1 block of a 4x4x8 slice. The times are simulated.
32 devices in a mesh: data: 1 (over z), inner: 4 (over y), stage: 8 (over x, core).
Axes of the slice: x: 4, y: 4, z: 1, core: 2. Of those that a mesh axis runs over, the one named last changes fastest.
The devices are a block of a 4x4x8 slice.
Arguments:
- x: bfloat16 [64, 128, 768], P(('data', 'stage', 'inner'))
- g: bfloat16 [64, 128, 768], P(('data', 'stage', 'inner'))
- w1: bfloat16 [1, 8, 1, 768, 3072], P(None, 'stage', None, None, 'inner')
- w2: bfloat16 [1, 8, 1, 3072, 768], P(None, 'stage', None, 'inner')
Outputs:
- output 1: bfloat16 [64, 128, 768], P(('data', 'stage', 'inner'))
- output 2: bfloat16 [64, 128, 768], P(('data', 'stage', 'inner'))
- output 3: float32 [1, 8, 1, 768, 3072], P('data', 'stage', None, None, 'inner')
- output 4: float32 [1, 8, 1, 3072, 768], P('data', 'stage', None, 'inner')
All inputs are finite; a program needn't handle non-finite values.
Results may differ from a plain program's by a relative error of at most 0.0156898.
Values are sent between devices in bfloat16 or wider.
A program may use at most 768 MiB of HBM per device.

v0:
```python
import jax
import jax.numpy as jnp
from jax import lax
from jax.sharding import PartitionSpec as P


def _gelu(u):
    return jax.nn.gelu(u, approximate=True)


def solution(mesh):
    ns = mesh.shape['stage']
    act = P(('data', 'stage', 'inner'), None, None)
    s1 = P(None, 'stage', None, None, 'inner')
    s2 = P(None, 'stage', None, 'inner', None)
    o1 = P('data', 'stage', None, None, 'inner')
    o2 = P('data', 'stage', None, 'inner', None)
    up = [(i, (i + 1) % ns) for i in range(ns)]
    down = [(i, (i - 1) % ns) for i in range(ns)]
    f32 = jnp.float32
    bf16 = jnp.bfloat16

    def body(x, g, w1, w2):
        md, b, d = x.shape
        nv, _, nk, _, _ = w1.shape
        n = ns * md
        total = nv * n
        ticks = total + ns - 1
        s = lax.axis_index('stage')
        w1f = lax.all_gather(w1[:, 0], 'inner', axis=3, tiled=True)
        w2f = lax.all_gather(w2[:, 0], 'inner', axis=2, tiled=True)
        xa = lax.all_gather(x, 'stage', axis=0, tiled=True)
        ga = lax.all_gather(g, 'stage', axis=0, tiled=True)
        ff = w1f.shape[-1]

        def store(buf, t, inc):
            ip = t - ns
            pm = jnp.clip(ip, 0, total - 1) % n
            new = jnp.where(ip >= 0, inc, buf[pm])
            return lax.dynamic_update_slice(buf, new[None], (pm, 0, 0))

        def keep(arr, v, m, val, ok):
            idx = (v, 0, m, 0, 0)
            old = lax.dynamic_slice(arr, idx, (1, nk, 1) + val.shape[1:])
            return lax.dynamic_update_slice(arr, jnp.where(ok, val[None, :, None], old), idx)

        def fwd_tick(carry, t):
            inc, buf, saved, yout = carry
            buf = store(buf, t, inc)
            i = t - s
            valid = (i >= 0) & (i < total)
            ic = jnp.clip(i, 0, total - 1)
            m = ic % n
            v = ic // n
            h = jnp.where(s == 0, jnp.where(v == 0, xa[m], buf[m]), inc)
            w1c = w1f[v]
            w2c = w2f[v]
            hs = []
            for j in range(nk):
                hs.append(h)
                u = jnp.dot(h, w1c[j], preferred_element_type=f32)
                a = _gelu(u).astype(bf16)
                h = (h.astype(f32) + jnp.dot(a, w2c[j], preferred_element_type=f32)).astype(bf16)
            saved = keep(saved, v, m, jnp.stack(hs), valid)
            last = valid & (s == ns - 1) & (v == nv - 1)
            yout = lax.dynamic_update_slice(yout, jnp.where(last, h, yout[m])[None], (m, 0, 0))
            inc = lax.ppermute(h, 'stage', up)
            return (inc, buf, saved, yout), None

        zb = jnp.zeros((b, d), bf16)
        zn = jnp.zeros((n, b, d), bf16)
        ts = jnp.arange(ticks)
        init = (zb, zn, jnp.zeros((nv, nk, n, b, d), bf16), zn)
        (_, _, saved, yout), _ = lax.scan(fwd_tick, init, ts)

        def bwd_tick(carry, t):
            inc, buf, ta, tu, tg, dxo = carry
            buf = store(buf, t, inc)
            i = t - (ns - 1 - s)
            valid = (i >= 0) & (i < total)
            ic = jnp.clip(i, 0, total - 1)
            m = ic % n
            v = nv - 1 - ic // n
            dh = jnp.where(s == ns - 1, jnp.where(v == nv - 1, ga[m], buf[m]), inc)
            w1c = w1f[v]
            w2c = w2f[v]
            hv = lax.dynamic_slice(saved, (v, 0, m, 0, 0), (1, nk, 1, b, d))[0, :, 0]
            la = [None] * nk
            lu = [None] * nk
            lg = [None] * nk
            for j in reversed(range(nk)):
                u = jnp.dot(hv[j], w1c[j], preferred_element_type=f32)
                gv, gvjp = jax.vjp(_gelu, u)
                la[j] = gv.astype(bf16)
                e = jnp.dot(dh, w2c[j].T, preferred_element_type=f32)
                du = gvjp(e)[0].astype(bf16)
                lu[j] = du
                lg[j] = dh
                dh = (dh.astype(f32) + jnp.dot(du, w1c[j].T, preferred_element_type=f32)).astype(bf16)
            ta = keep(ta, v, m, jnp.stack(la), valid)
            tu = keep(tu, v, m, jnp.stack(lu), valid)
            tg = keep(tg, v, m, jnp.stack(lg), valid)
            first = valid & (s == 0) & (v == 0)
            dxo = lax.dynamic_update_slice(dxo, jnp.where(first, dh, dxo[m])[None], (m, 0, 0))
            inc = lax.ppermute(dh, 'stage', down)
            return (inc, buf, ta, tu, tg, dxo), None

        zf = jnp.zeros((nv, nk, n, b, ff), bf16)
        init = (zb, zn, zf, zf, jnp.zeros((nv, nk, n, b, d), bf16), zn)
        (_, _, ta, tu, tg, dxo), _ = lax.scan(bwd_tick, init, ts)
        dn = (((2, 3), (2, 3)), ((0, 1), (0, 1)))
        dw1a = lax.dot_general(saved, tu, dn, preferred_element_type=f32)
        dw2a = lax.dot_general(ta, tg, dn, preferred_element_type=f32)
        y = lax.psum_scatter(jnp.where(s == ns - 1, yout, jnp.zeros_like(yout)), 'stage', scatter_dimension=0, tiled=True)
        dx = lax.psum_scatter(jnp.where(s == 0, dxo, jnp.zeros_like(dxo)), 'stage', scatter_dimension=0, tiled=True)
        dw1 = lax.psum_scatter(dw1a, 'inner', scatter_dimension=3, tiled=True)[:, None]
        dw2 = lax.psum_scatter(dw2a, 'inner', scatter_dimension=2, tiled=True)[:, None]
        return y, dx, dw1, dw2

    return jax.shard_map(body, mesh=mesh, in_specs=(act, act, s1, s2), out_specs=(act, act, o1, o2), check_vma=False)
```

profile of v0, /device:TPU:103, one launch (start us, length us, event | category | flops | bytes accessed | tf_op | source)
XLA Modules:
  0.0 1333.4 jit_solution(15545672888032173647)
XLA Ops:
  10.3 26.4 %all-gather.7.cloned.1.call-done = bf16[16,128,768]{2,1,0:T(8,128)(2,1)} async-done(((bf16[2,128,768]{2,1,0:T(8,128)(2,1)}), bf16[16,128,768]{2,1,0:T(8,128)(2,1)}) %all-gather.7.cloned.1.call-update) | async-done | bytes 3145744 | tf_op jit(solution)/shard_map/all_gather | solution.py:32
  36.7 51.9 %all-gather.11.cloned.1.call-done = bf16[1,1,1,768,3072]{4,3,2,1,0:T(8,128)(2,1)} async-done(((bf16[1,1,1,768,768]{4,3,2,1,0:T(8,128)(2,1)}), bf16[1,1,1,768,3072]{4,3,2,1,0:T(8,128)(2,1)}) %all-gather.11.cloned.1.call-update) | async-done | bytes 4718608 | tf_op jit(solution)/shard_map/all_gather | solution.py:30
  88.6 52.0 %all-gather.13.cloned.1.call-done = bf16[1,1,1,3072,768]{4,3,2,1,0:T(8,128)(2,1)} async-done(((bf16[1,1,1,768,768]{4,3,2,1,0:T(8,128)(2,1)}), bf16[1,1,1,3072,768]{4,3,2,1,0:T(8,128)(2,1)}) %all-gather.13.cloned.1.call-update) | async-done | bytes 4718608 | tf_op jit(solution)/shard_map/all_gather | solution.py:31
  144.9 416.4 %while.40 = (s32[]{:T(128)}, bf16[128,768]{1,0:T(8,128)(2,1)S(1)}, bf16[16,128,768]{2,1,0:T(8,128)(2,1)}, bf16[1,1,16,128,768]{4,3,2,1,0:T(8,128)(2,1)}, bf16[16...) while((s32[]{:T(128)}, bf16[128,768]{1,0:T(8,128)(2,1)S(1)}, ...), condition=%wide.region_1.2_spmd, body=%wide.region_0.1_spmd.sunk | while | flops 1212284928 | bytes 13763679 | solution.py:74
  157.7 6.8 collective-permute-done
  579.9 534.3 %while.41 = (s32[]{:T(128)}, bf16[128,768]{1,0:T(8,128)(2,1)S(1)}, bf16[16,128,768]{2,1,0:T(8,128)(2,1)}, bf16[1,1,16,128,3072]{4,3,2,1,0:T(8,128)(2,1)}, bf16[1...) while((s32[]{:T(128)}, bf16[128,768]{1,0:T(8,128)(2,1)S(1)}, ...), condition=%wide.region_4.5_spmd, body=%wide.region_3.4_spmd.sunk | while | flops 1824915456 | bytes 54856420 | solution.py:110
  596.8 7.0 collective-permute-done.1
  620.8 6.3 collective-permute-done.1
  643.9 6.3 collective-permute-done.1
  667.1 6.3 collective-permute-done.1
  690.2 6.3 collective-permute-done.1
  713.4 6.3 collective-permute-done.1
  736.6 6.3 collective-permute-done.1
  759.8 6.3 collective-permute-done.1
  782.9 6.3 collective-permute-done.1
  806.1 6.3 collective-permute-done.1
  829.3 6.3 collective-permute-done.1
  852.5 6.3 collective-permute-done.1
  875.7 6.3 collective-permute-done.1
  898.8 6.3 collective-permute-done.1
  922.0 6.3 collective-permute-done.1
  945.2 6.3 collective-permute-done.1
  968.5 6.3 collective-permute-done.1
  991.7 6.3 collective-permute-done.1
  1014.9 6.3 collective-permute-done.1
  1038.2 6.3 collective-permute-done.1
  1061.4 6.3 collective-permute-done.1
  1084.6 6.3 collective-permute-done.1
  1117.9 15.2 %fusion.63 = f32[1,1,768,3072]{3,2,1,0:T(8,128)} fusion(bf16[1,1,16,128,3072]{4,3,2,1,0:T(8,128)(2,1)} %get-tuple-element.329, bf16[1,1,16,128,768]{4,3,2,1,0:T(8,128)(2,1)S(1)} %copy-done.1), kind=kOutput, calls=%fused_computation.67 | convolution fusion | flops 9663676416 | bytes 25165824 | tf_op jit(solution)/shard_map/dot_general | solution.py:112
  1135.1 15.2 %fusion.60 = f32[1,1,3072,768]{3,2,1,0:T(8,128)} fusion(bf16[1,1,16,128,3072]{4,3,2,1,0:T(8,128)(2,1)} %get-tuple-element.330, bf16[1,1,16,128,768]{4,3,2,1,0:T(8,128)(2,1)S(1)} %copy-done), kind=kOutput, calls=%fused_computation.66 | convolution fusion | flops 9663676416 | bytes 25165824 | tf_op jit(solution)/shard_map/dot_general | solution.py:113
  1150.4 86.9 %reduce-scatter.9.cloned.1.call-done = f32[1,1,768,768]{3,2,1,0:T(8,128)} async-done(((f32[1,1,768,3072]{3,2,1,0:T(8,128)}), f32[1,1,768,768]{3,2,1,0:T(8,128)}) %reduce-scatter.9.cloned.1.call-update) | async-done | bytes 2359312 | tf_op jit(solution)/shard_map/reduce_scatter | solution.py:116
  1237.4 89.2 %reduce-scatter.11.cloned.1.call-done = f32[1,1,768,768]{3,2,1,0:T(8,128)} async-done(((f32[1,1,3072,768]{3,2,1,0:T(8,128)}), f32[1,1,768,768]{3,2,1,0:T(8,128)}) %reduce-scatter.11.cloned.1.call-update) | async-done | bytes 2359312 | tf_op jit(solution)/shard_map/reduce_scatter | solution.py:117
  (612 shorter events, 774.1 us)
Async XLA Ops:
  7.2 29.6 %all-gather.7.cloned.1.call-start = ((), (), s32[]{:S(2)}) async-start(), calls=%async_computation.4 | async-start | bytes 3538944 | tf_op jit(solution)/shard_map/all_gather | solution.py:32
  8.0 80.6 %all-gather.11.cloned.1.call-start = ((), (), s32[]{:S(2)}) async-start(), calls=%async_computation.10 | async-start | bytes 5898240 | tf_op jit(solution)/shard_map/all_gather | solution.py:30
  8.8 131.8 %all-gather.13.cloned.1.call-start = ((), (), s32[]{:S(2)}) async-start(), calls=%async_computation.11 | async-start | bytes 5898240 | tf_op jit(solution)/shard_map/all_gather | solution.py:31
  9.6 553.7 %all-gather.9.cloned.1.call-start = ((), (), s32[]{:S(2)}) async-start(), calls=%async_computation.6 | async-start | bytes 3538944 | tf_op jit(solution)/shard_map/all_gather | solution.py:33
  10.2 1140.2 %reduce-scatter.5.cloned.1.call-start = ((), (), s32[]{:S(2)}) async-start(), calls=%async_computation.5 | async-start | bytes 3538944 | tf_op jit(solution)/shard_map/reduce_scatter | solution.py:114
  156.6 7.9 collective-permute-start
  563.2 587.3 %reduce-scatter.7.cloned.1.call-start = ((), (), s32[]{:S(2)}) async-start(), calls=%async_computation.7 | async-start | bytes 3538944 | tf_op jit(solution)/shard_map/reduce_scatter | solution.py:115
  596.7 7.1 collective-permute-start.1
  620.7 6.4 collective-permute-start.1
  643.9 6.4 collective-permute-start.1
  667.0 6.4 collective-permute-start.1
  690.2 6.4 collective-permute-start.1
  713.3 6.4 collective-permute-start.1
  736.5 6.4 collective-permute-start.1
  759.7 6.4 collective-permute-start.1
  782.8 6.4 collective-permute-start.1
  806.0 6.4 collective-permute-start.1
  829.2 6.4 collective-permute-start.1
  852.4 6.4 collective-permute-start.1
  875.6 6.4 collective-permute-start.1
  898.8 6.4 collective-permute-start.1
  921.9 6.4 collective-permute-start.1
  945.2 6.4 collective-permute-start.1
  968.4 6.4 collective-permute-start.1
  991.6 6.4 collective-permute-start.1
  1014.9 6.4 collective-permute-start.1
  1038.1 6.4 collective-permute-start.1
  1061.3 6.4 collective-permute-start.1
  1084.6 6.4 collective-permute-start.1
  1107.8 6.4 collective-permute-start.1
  1116.1 121.2 %reduce-scatter.9.cloned.1.call-start = ((), (), s32[]{:S(2)}) async-start(), calls=%async_computation.8 | async-start | bytes 11796480 | tf_op jit(solution)/shard_map/reduce_scatter | solution.py:116
  1133.2 193.3 %reduce-scatter.11.cloned.1.call-start = ((), (), s32[]{:S(2)}) async-start(), calls=%async_computation.9 | async-start | bytes 11796480 | tf_op jit(solution)/shard_map/reduce_scatter | solution.py:117
  (116 other events, 773.0 us)
Sparse Core Ops, SparseCore 0:
  9.6 27.0 all-gather.6
  38.3 50.2 all-gather.10
  90.2 50.3 all-gather.12
  142.0 26.2 all-gather.8
  563.3 32.2 reduce-scatter.4
  1116.2 31.0 reduce-scatter.6
  1150.2 87.0 reduce-scatter.8
  1240.3 86.2 reduce-scatter.10
where the time goes:
time: 1340 us; the launch traced here: 1330 us
  waiting for transfers between devices  518 us (39%)
  matrix products  425 us (32%)
  other arithmetic  130 us (10%)
  local copies, waits for them, and re-layouts  98.5 us (7%)
  starting transfers between devices  84.8 us (6%)
  loops' own time  62.5 us (5%)
  between operations  14.2 us (1%)
    ppermute x23, waiting for transfers between devices, bwd_tick(): inc = lax.ppermute(dh, 'stage', down)  145 us
    dot_general x23, matrix products, fwd_tick(): jnp.dot(a, w2c[j], preferred_element_type=f32)  142 us
    dot_general x23, matrix products, bwd_tick(): u = jnp.dot(hv[j], w1c[j], preferred_element_type=f32)  118 us
    dot_general x23, matrix products, bwd_tick(): e = jnp.dot(dh, w2c[j].T, preferred_element_type=f32)  96.7 us
    dynamic_update_slice x46, other arithmetic, keep(): lax.dynamic_update_slice(arr, jnp.where(ok, val[None, :, None], old), idx)  90.8 us
    reduce_scatter x1, waiting for transfers between devices, body(): lax.psum_scatter(dw2a, 'inner', scatter_dimension=2, tiled=True)[:, None]  89.2 us
    reduce_scatter x1, waiting for transfers between devices, body(): lax.psum_scatter(dw1a, 'inner', scatter_dimension=3, tiled=True)[:, None]  86.9 us
    ppermute x23, starting transfers between devices, fwd_tick(): inc = lax.ppermute(h, 'stage', up)  82.6 us
  transfers between devices with their start and end apart: 54, of which 51 were waited for; matrix products, arithmetic and copies ran while one was open for 49% of the time, Pallas kernels for 0%

commit v1 on v0

v1 whole, which is shorter than its diff:
```python
import functools

import jax
import jax.numpy as jnp
from jax import lax
from jax.experimental import pallas as pl
from jax.experimental.pallas import tpu as pltpu
from jax.sharding import PartitionSpec as P

MESH = pl.DeviceIdType.MESH
F32 = jnp.float32
BF16 = jnp.bfloat16
C0 = 0.7978845608
C1 = 0.044715


def _dot(a, b):
    return jnp.dot(a, b, preferred_element_type=F32)


def _dot_t(a, b):
    return lax.dot_general(a, b, (((1,), (1,)), ((), ())), preferred_element_type=F32)


def _remote(src, dst, ssem, rsem, dev):
    return pltpu.make_async_remote_copy(src_ref=src, dst_ref=dst, send_sem=ssem, recv_sem=rsem, device_id=dev, device_id_type=MESH)


def _pipe_kernel(ns, ni, md, x_ref, g_ref, w1_ref, w2_ref,
                 y_ref, dx_ref, ht_ref, gt_ref, a_ref, du_ref, gp_ref,
                 w1f, w2f, hbuf, gbuf, hout, gout, htv, gtv, abuf, dubuf, gpbuf,
                 wsend, wrecv, wloc, xsend, hrecv, grecv, hsend, gsend, yrecv, dxrecv,
                 htsem, gtsem, asem, dusem, gpsem):
    s = lax.axis_index('stage')
    i = lax.axis_index('inner')
    n = ns * md
    b = x_ref.shape[1]
    right = lax.rem(i + 1, ni)
    left = lax.rem(i + ni - 1, ni)
    opp = lax.rem(i + 2, ni)

    barrier = pltpu.get_barrier_semaphore()
    for k in range(1, ns):
        pl.semaphore_signal(barrier, inc=1, device_id={'stage': lax.rem(s + k, ns)}, device_id_type=MESH)
    for nb in (left, right):
        pl.semaphore_signal(barrier, inc=1, device_id={'inner': nb}, device_id_type=MESH)

    own1 = pltpu.make_async_copy(w1_ref, w1f.at[i], wloc.at[0])
    own2 = pltpu.make_async_copy(w2_ref, w2f.at[i], wloc.at[1])
    own1.start()
    own2.start()
    pl.semaphore_wait(barrier, ns + 1)

    rs = [_remote(w1_ref, w1f.at[i], wsend.at[0], wrecv.at[0], {'inner': right}),
          _remote(w2_ref, w2f.at[i], wsend.at[1], wrecv.at[1], {'inner': right})]
    ls = [_remote(w2_ref, w2f.at[i], wsend.at[3], wrecv.at[3], {'inner': left}),
          _remote(w1_ref, w1f.at[i], wsend.at[4], wrecv.at[4], {'inner': left})]
    rs[0].start()
    ls[0].start()
    rs[1].start()
    ls[1].start()

    for k in range(md):
        m = s * md + k

        @pl.when(s == 0)
        def _():
            pltpu.make_async_copy(x_ref.at[k], hbuf.at[m], hrecv.at[m]).start()

        @pl.when(s != 0)
        def _():
            _remote(x_ref.at[k], hbuf.at[m], xsend.at[k], hrecv.at[m], {'stage': 0}).start()

    for k in range(md):
        m = s * md + k

        @pl.when(s == ns - 1)
        def _():
            pltpu.make_async_copy(g_ref.at[k], gbuf.at[m], grecv.at[m]).start()

        @pl.when(s != ns - 1)
        def _():
            _remote(g_ref.at[k], gbuf.at[m], xsend.at[md + k], grecv.at[m], {'stage': ns - 1}).start()

    pltpu.make_async_copy(w1f.at[left], w1f.at[left], wrecv.at[0]).wait()
    fr = _remote(w1f.at[left], w1f.at[left], wsend.at[2], wrecv.at[2], {'inner': right})
    fr.start()
    pltpu.make_async_copy(w2f.at[right], w2f.at[right], wrecv.at[3]).wait()
    fl = _remote(w2f.at[right], w2f.at[right], wsend.at[5], wrecv.at[5], {'inner': left})
    fl.start()
    own1.wait()
    own2.wait()
    pltpu.make_async_copy(w2f.at[left], w2f.at[left], wrecv.at[1]).wait()
    pltpu.make_async_copy(w1f.at[right], w1f.at[right], wrecv.at[4]).wait()
    pltpu.make_async_copy(w1f.at[opp], w1f.at[opp], wrecv.at[2]).wait()
    pltpu.make_async_copy(w2f.at[opp], w2f.at[opp], wrecv.at[5]).wait()

    def fwd(m, c):
        slot = lax.rem(m, 2)
        col = pl.ds(pl.multiple_of(m * b, b), b)
        pltpu.make_async_copy(hbuf.at[m], hbuf.at[m], hrecv.at[m]).wait()

        @pl.when(m >= 2)
        def _():
            pltpu.make_async_copy(abuf.at[slot], a_ref.at[:, m - 2], asem.at[slot]).wait()
            pltpu.make_async_copy(gpbuf.at[slot], gp_ref.at[:, m - 2], gpsem.at[slot]).wait()

        h = hbuf[m]
        for q in range(ni):
            u = _dot(h, w1f[q])
            u2 = u * u
            t = jnp.tanh(u * (C0 + (C0 * C1) * u2))
            p = 0.5 + 0.5 * t
            hu = 0.5 * u
            abuf[slot, q] = (u * p).astype(BF16)
            gpbuf[slot, q] = p + hu * (1.0 - t * t) * (C0 + (3.0 * C0 * C1) * u2)
        acc = _dot(abuf[slot, 0], w2f[0])
        for q in range(1, ni):
            acc = acc + _dot(abuf[slot, q], w2f[q])
        hout[m] = (h.astype(F32) + acc).astype(BF16)
        home = m // md
        kk = lax.rem(m, md)

        @pl.when(s < ns - 1)
        def _():
            _remote(hout.at[m], hbuf.at[m], hsend, hrecv.at[m], {'stage': lax.rem(s + 1, ns)}).start()

        @pl.when((s == ns - 1) & (home != ns - 1))
        def _():
            _remote(hout.at[m], y_ref.at[kk], hsend, yrecv.at[kk], {'stage': home}).start()

        @pl.when((s == ns - 1) & (home == ns - 1))
        def _():
            pltpu.make_async_copy(hout.at[m], y_ref.at[kk], hsend).start()

        pltpu.make_async_copy(abuf.at[slot], a_ref.at[:, m], asem.at[slot]).start()
        pltpu.make_async_copy(gpbuf.at[slot], gp_ref.at[:, m], gpsem.at[slot]).start()
        htv[:, col] = h.T
        pltpu.make_async_copy(htv.at[:, col], ht_ref.at[:, col], htsem).start()
        return c

    lax.fori_loop(0, n, fwd, 0)
    for k in range(2):
        pltpu.make_async_copy(abuf.at[k], a_ref.at[:, n - 2 + k], asem.at[k]).wait()
        pltpu.make_async_copy(gpbuf.at[k], gp_ref.at[:, n - 2 + k], gpsem.at[k]).wait()
    for k in range(2):
        pltpu.make_async_copy(gp_ref.at[:, k], gpbuf.at[k], gpsem.at[k]).start()

    def bwd(m, c):
        slot = lax.rem(m, 2)
        col = pl.ds(pl.multiple_of(m * b, b), b)
        pltpu.make_async_copy(gp_ref.at[:, m], gpbuf.at[slot], gpsem.at[slot]).wait()
        pltpu.make_async_copy(gbuf.at[m], gbuf.at[m], grecv.at[m]).wait()

        @pl.when(m >= 2)
        def _():
            pltpu.make_async_copy(dubuf.at[slot], du_ref.at[:, m - 2], dusem.at[slot]).wait()

        g = gbuf[m]
        for q in range(ni):
            e = _dot_t(g, w2f[q])
            dubuf[slot, q] = (e * gpbuf[slot, q]).astype(BF16)
        acc = _dot_t(dubuf[slot, 0], w1f[0])
        for q in range(1, ni):
            acc = acc + _dot_t(dubuf[slot, q], w1f[q])
        gout[m] = (g.astype(F32) + acc).astype(BF16)
        home = m // md
        kk = lax.rem(m, md)

        @pl.when(s > 0)
        def _():
            _remote(gout.at[m], gbuf.at[m], gsend, grecv.at[m], {'stage': lax.rem(s + ns - 1, ns)}).start()

        @pl.when((s == 0) & (home != 0))
        def _():
            _remote(gout.at[m], dx_ref.at[kk], gsend, dxrecv.at[kk], {'stage': home}).start()

        @pl.when((s == 0) & (home == 0))
        def _():
            pltpu.make_async_copy(gout.at[m], dx_ref.at[kk], gsend).start()

        pltpu.make_async_copy(dubuf.at[slot], du_ref.at[:, m], dusem.at[slot]).start()

        @pl.when(m < n - 2)
        def _():
            pltpu.make_async_copy(gp_ref.at[:, m + 2], gpbuf.at[slot], gpsem.at[slot]).start()

        gtv[:, col] = g.T
        pltpu.make_async_copy(gtv.at[:, col], gt_ref.at[:, col], gtsem).start()
        return c

    lax.fori_loop(0, n, bwd, 0)

    for k in range(2):
        pltpu.make_async_copy(dubuf.at[k], du_ref.at[:, n - 2 + k], dusem.at[k]).wait()
    pltpu.make_async_copy(htv, ht_ref, htsem).wait()
    pltpu.make_async_copy(gtv, gt_ref, gtsem).wait()
    pltpu.make_async_copy(hout, hout, hsend).wait()
    pltpu.make_async_copy(gout, gout, gsend).wait()
    for r in rs + ls + [fr, fl]:
        r.wait_send()
    for k in range(md):
        @pl.when(s != 0)
        def _():
            pltpu.make_async_copy(x_ref.at[k], x_ref.at[k], xsend.at[k]).wait()
            pltpu.make_async_copy(dx_ref.at[k], dx_ref.at[k], dxrecv.at[k]).wait()

        @pl.when(s != ns - 1)
        def _():
            pltpu.make_async_copy(g_ref.at[k], g_ref.at[k], xsend.at[md + k]).wait()
            pltpu.make_async_copy(y_ref.at[k], y_ref.at[k], yrecv.at[k]).wait()


def _wgrad_kernel(ni, nr, ht_ref, gt_ref, a_ref, du_ref, o1_ref, o2_ref,
                  hv, gv, dv, av, s1, s2, r1, r2,
                  lsem, dsem, snd1, snd2, rcv1, rcv2):
    i = lax.axis_index('inner')
    right = lax.rem(i + 1, ni)
    left = lax.rem(i + ni - 1, ni)
    barrier = pltpu.get_barrier_semaphore()
    for nb in (left, right):
        pl.semaphore_signal(barrier, inc=1, device_id={'inner': nb}, device_id_type=MESH)
    ch = pltpu.make_async_copy(ht_ref, hv, lsem.at[0])
    cg = pltpu.make_async_copy(gt_ref, gv, lsem.at[1])

    def loads(t):
        c1 = lax.rem(i + 2 * ni - 1 - t, ni)
        c2 = lax.rem(i + 1 + t, ni)
        return (pltpu.make_async_copy(du_ref.at[c1], dv.at[t % 2], dsem.at[0, t % 2]),
                pltpu.make_async_copy(a_ref.at[c2], av.at[t % 2], dsem.at[1, t % 2]))

    cps = loads(0)
    ch.start()
    cps[0].start()
    cg.start()
    cps[1].start()
    pl.semaphore_wait(barrier, 2)
    rows = s1.shape[1]
    k = dv.shape[1] * dv.shape[2]
    d = dv.shape[3]
    for t in range(ni):
        nxt = loads(t + 1) if t + 1 < ni else None
        if nxt is not None:
            nxt[0].start()
            nxt[1].start()
        if t == 0:
            ch.wait()
        cps[0].wait()
        if t == 0:
            cg.wait()
        cps[1].wait()
        slot = t % 2

        def block(r, c):
            row = pl.ds(pl.multiple_of(r * rows, rows), rows)
            p1 = _dot(hv[row, :], dv[slot].reshape(k, d))
            if t == 0:
                src1 = s1.at[r]
                s1[r] = p1
            else:
                src1 = r1.at[t - 1, r]
                pltpu.make_async_copy(src1, src1, rcv1.at[t - 1, r]).wait()
                if t < ni - 1:
                    r1[t - 1, r] = r1[t - 1, r] + p1
                else:
                    o1_ref[row, :] = r1[t - 1, r] + p1
            if t < ni - 1:
                _remote(src1, r1.at[t, r], snd1, rcv1.at[t, r], {'inner': right}).start()
            p2 = _dot(gv[row, :], av[slot].reshape(k, d))
            if t == 0:
                src2 = s2.at[r]
                s2[r] = p2
            else:
                src2 = r2.at[t - 1, r]
                pltpu.make_async_copy(src2, src2, rcv2.at[t - 1, r]).wait()
                if t < ni - 1:
                    r2[t - 1, r] = r2[t - 1, r] + p2
                else:
                    o2_ref[:, row] = (r2[t - 1, r] + p2).T
            if t < ni - 1:
                _remote(src2, r2.at[t, r], snd2, rcv2.at[t, r], {'inner': left}).start()
            return c

        lax.fori_loop(0, nr, block, 0)
        cps = nxt
    for sem in (snd1, snd2):
        pltpu.make_async_copy(r1, r1, sem).wait()


def solution(mesh):
    ns = mesh.shape['stage']
    ni = mesh.shape['inner']
    act = P(('data', 'stage', 'inner'), None, None)
    s1 = P(None, 'stage', None, None, 'inner')
    s2 = P(None, 'stage', None, 'inner', None)
    o1 = P('data', 'stage', None, None, 'inner')
    o2 = P('data', 'stage', None, 'inner', None)
    any_ = pl.BlockSpec(memory_space=pl.ANY)
    vmem = pl.BlockSpec(memory_space=pltpu.VMEM)
    dma = pltpu.SemaphoreType.DMA

    def body(x, g, w1, w2):
        md, b, d = x.shape
        f = w1.shape[-1]
        n = ns * md
        sds = jax.ShapeDtypeStruct
        y, dx, ht, gt, a, du, _ = pl.pallas_call(
            functools.partial(_pipe_kernel, ns, ni, md),
            out_shape=(sds((md, b, d), BF16), sds((md, b, d), BF16), sds((d, n * b), BF16), sds((d, n * b), BF16),
                       sds((ni, n, b, f), BF16), sds((ni, n, b, f), BF16), sds((ni, n, b, f), F32)),
            in_specs=[any_] * 4,
            out_specs=(any_,) * 7,
            scratch_shapes=[
                pltpu.VMEM((ni, d, f), BF16), pltpu.VMEM((ni, f, d), BF16),
                pltpu.VMEM((n, b, d), BF16), pltpu.VMEM((n, b, d), BF16),
                pltpu.VMEM((n, b, d), BF16), pltpu.VMEM((n, b, d), BF16),
                pltpu.VMEM((d, n * b), BF16), pltpu.VMEM((d, n * b), BF16),
                pltpu.VMEM((2, ni, b, f), BF16), pltpu.VMEM((2, ni, b, f), BF16),
                pltpu.VMEM((2, ni, b, f), F32),
                dma((6,)), dma((6,)), dma((2,)), dma((2 * md,)), dma((n,)), dma((n,)),
                dma(()), dma(()), dma((md,)), dma((md,)),
                dma(()), dma(()), dma((2,)), dma((2,)), dma((2,)),
            ],
            compiler_params=pltpu.CompilerParams(collective_id=0, has_side_effects=True, vmem_limit_bytes=60 * 2**20),
            name='pipe',
        )(x, g, w1[0, 0, 0], w2[0, 0, 0])
        nr = d // b
        dw1, dw2 = pl.pallas_call(
            functools.partial(_wgrad_kernel, ni, nr),
            out_shape=(sds((d, f), F32), sds((f, d), F32)),
            in_specs=[any_] * 4,
            out_specs=(vmem, vmem),
            scratch_shapes=[
                pltpu.VMEM((d, n * b), BF16), pltpu.VMEM((d, n * b), BF16),
                pltpu.VMEM((2, n, b, f), BF16), pltpu.VMEM((2, n, b, f), BF16),
                pltpu.VMEM((nr, b, f), F32), pltpu.VMEM((nr, b, f), F32),
                pltpu.VMEM((ni - 1, nr, b, f), F32), pltpu.VMEM((ni - 1, nr, b, f), F32),
                dma((2,)), dma((2, 2)), dma(()), dma(()),
                dma((ni - 1, nr)), dma((ni - 1, nr)),
            ],
            compiler_params=pltpu.CompilerParams(collective_id=1, has_side_effects=True, vmem_limit_bytes=60 * 2**20),
            name='wgrad',
        )(ht, gt, a, du)
        return y, dx, dw1[None, None, None], dw2[None, None, None]

    return jax.shard_map(body, mesh=mesh, in_specs=(act, act, s1, s2), out_specs=(act, act, o1, o2), check_vma=False)
```

time: 1340 us -> 406 us (0.30)
  waiting for transfers between devices: 518 us -> 0 us
  matrix products: 425 us -> 0 us
  Pallas kernels: 0 us -> 399 us
  other arithmetic: 130 us -> 0 us
  local copies, waits for them, and re-layouts: 98.5 us -> 6.28 us
  starting transfers between devices: 84.8 us -> 0 us
  loops' own time: 62.5 us -> 0 us
  between operations: 14.2 us -> 0.67 us
    dot_general x94 -> x0, matrix products: 425 us -> none  [the longest x23 142 us: fwd_tick(): jnp.dot(a, w2c[j], preferred_element_type=f32)]
    pallas_call x0 -> x2, Pallas kernels: none -> 399 us  [the longest x1 243 us: body(): pl.pallas_call(functools.partial(_pipe_kernel, ns, ni, md), out_shape=(sd...]
    ppermute x46 -> x0, waiting for transfers between devices: 209 us -> none  [the longest x23 145 us: bwd_tick(): inc = lax.ppermute(dh, 'stage', down)]
    reduce_scatter x4 -> x0, waiting for transfers between devices: 176 us -> none  [the longest x1 89.2 us: body(): lax.psum_scatter(dw2a, 'inner', scatter_dimension=2, tiled=True)[:, None]]
    all_gather x4 -> x0, waiting for transfers between devices: 130 us -> none  [the longest x1 52 us: body(): w2f = lax.all_gather(w2[:, 0], 'inner', axis=2, tiled=True)]
    dynamic_update_slice x92 -> x0, other arithmetic: 126 us -> none  [the longest x46 90.8 us: keep(): lax.dynamic_update_slice(arr, jnp.where(ok, val[None, :, None], old), idx)]
    ppermute x46 -> x0, starting transfers between devices: 84.1 us -> none  [the longest x23 82.6 us: fwd_tick(): inc = lax.ppermute(h, 'stage', up)]
    dynamic_slice x92 -> x0, local copies, waits for them, and re-layouts: 73.8 us -> none  [the longest x46 47.1 us: store(): new = jnp.where(ip >= 0, inc, buf[pm])]
  transfers between devices with their start and end apart: 54 -> 0, of which waited for: 51 -> 0; matrix products, arithmetic and copies ran while one was open for 49% -> 0% of each run, Pallas kernels for 0% -> 0%
where the time goes in v1:
time: 406 us
  Pallas kernels  399 us (98%)
  local copies, waits for them, and re-layouts  6.28 us (2%)
    pallas_call x1, Pallas kernels, body(): pl.pallas_call(functools.partial(_pipe_kernel, ns, ni, md), out_shape=(sd...  243 us
    pallas_call x1, Pallas kernels, body(): pl.pallas_call(functools.partial(_wgrad_kernel, ni, nr), out_shape=(sds((...  156 us

profile of v1, /device:TPU:103, one launch (start us, length us, event | category | flops | bytes accessed | tf_op | source)
XLA Modules:
  0.0 406.2 jit_solution(13566411030835834404)
XLA Ops:
  0.6 243.0 %pipe.1 = (bf16[2,128,768]{2,1,0:T(8,128)(2,1)}, bf16[2,128,768]{2,1,0:T(8,128)(2,1)}, bf16[768,2048]{1,0:T(8,128)(2,1)}, bf16[768,2048]{1,0:T(8,128)(2,1)}, bf1...) custom-call(bf16[2,128,768]{2,1,0:T(8,128)(2,1)} %x_ref.1, ...), custom_call_target="tpu_custom_call" | custom-call | tf_op jit(solution)/shard_map/pipe/pallas_call | solution.py:307
  243.6 0.0 copy-start.2
  243.6 0.0 copy-start.1
  243.6 156.2 %wgrad.1 = (f32[768,768]{1,0:T(8,128)}, f32[768,768]{1,0:T(8,128)}) custom-call(bf16[768,2048]{1,0:T(8,128)(2,1)} %get-tuple-element.14.ht_ref, bf16[768,2048]{1,0:T(8,128)(2,1)} %get-tuple-element.15.gt_ref, bf16[4,16,128,768]{3,2,1,0:T(8,128)(2,1)} %get-tuple-element.16.a_ref, bf16[4,16,128,768]{3,2,1,0:T(8,128)(2,1)} %get-tuple-element.17.du_ref), custom_call_target="tpu_custom_call" | custom-call | tf_op jit(solution)/shard_map/wgrad/pallas_call | solution.py:328
  399.9 0.0 copy-done.2
  399.9 0.7 copy.12
  400.6 0.0 copy-done.1
  400.6 0.7 copy.13
  401.4 0.0 copy-start
  401.4 3.4 copy.14
  404.8 0.0 copy-done
  404.8 1.4 copy.15
Async XLA Ops:
  243.6 156.3 %copy-start.2 = (bf16[2,128,768]{2,1,0:T(8,128)(2,1)S(1)}, bf16[2,128,768]{2,1,0:T(8,128)(2,1)}, u32[]{:S(2)}) copy-start(bf16[2,128,768]{2,1,0:T(8,128)(2,1)} %get-tuple-element.24) | copy-start | bytes 1179652
  243.6 157.0 %copy-start.1 = (bf16[2,128,768]{2,1,0:T(8,128)(2,1)S(1)}, bf16[2,128,768]{2,1,0:T(8,128)(2,1)}, u32[]{:S(2)}) copy-start(bf16[2,128,768]{2,1,0:T(8,128)(2,1)} %get-tuple-element.25) | copy-start | bytes 1179652
  401.4 3.4 copy-start

commit v2 on v1

v2 whole, which is shorter than its diff:
```python
import functools

import jax
import jax.numpy as jnp
from jax import lax
from jax.experimental import pallas as pl
from jax.experimental.pallas import tpu as pltpu
from jax.sharding import PartitionSpec as P

MESH = pl.DeviceIdType.MESH
F32 = jnp.float32
BF16 = jnp.bfloat16
C0 = 0.7978845608
C1 = 0.044715


def _dot(a, b):
    return jnp.dot(a, b, preferred_element_type=F32)


def _dot_t(a, b):
    return lax.dot_general(a, b, (((1,), (1,)), ((), ())), preferred_element_type=F32)


def _gate(u):
    return 0.5 + 0.5 * jnp.tanh(u * (C0 + (C0 * C1) * (u * u)))


def _slope(u, p):
    return p * (1.0 + ((1.0 - p) * u) * (2.0 * C0 + (6.0 * C0 * C1) * (u * u)))


def _remote(src, dst, ssem, rsem, dev):
    return pltpu.make_async_remote_copy(src_ref=src, dst_ref=dst, send_sem=ssem, recv_sem=rsem, device_id=dev, device_id_type=MESH)


def _pipe_kernel(ns, ni, md, x_ref, g_ref, w1_ref, w2_ref,
                 y_ref, dx_ref, hg_ref, a_ref, du_ref,
                 w1f, w2f, w1t, w2t, hbuf, gbuf, gp, htb, gtb, abuf, dubuf,
                 wsend, wrecv, wloc, xsend, hrecv, grecv, hsend, gsend, yrecv, dxrecv,
                 htsem, gtsem, asem, dusem, ygo):
    s = lax.axis_index('stage')
    i = lax.axis_index('inner')
    n = ns * md
    b, d = x_ref.shape[1:]
    f = w1_ref.shape[1]
    right = lax.rem(i + 1, ni)
    left = lax.rem(i + ni - 1, ni)
    opp = lax.rem(i + 2, ni)

    barrier = pltpu.get_barrier_semaphore()
    for k in range(1, ns):
        pl.semaphore_signal(barrier, inc=1, device_id={'stage': lax.rem(s + k, ns)}, device_id_type=MESH)
    for nb in (left, right):
        pl.semaphore_signal(barrier, inc=1, device_id={'inner': nb}, device_id_type=MESH)

    own1 = pltpu.make_async_copy(w1_ref, w1f.at[i], wloc.at[0])
    own2 = pltpu.make_async_copy(w2_ref, w2f.at[i], wloc.at[1])
    own1.start()
    own2.start()
    pl.semaphore_wait(barrier, ns + 1)

    rs = [_remote(w1_ref, w1f.at[i], wsend.at[0], wrecv.at[0], {'inner': right}),
          _remote(w2_ref, w2f.at[i], wsend.at[1], wrecv.at[1], {'inner': right})]
    ls = [_remote(w2_ref, w2f.at[i], wsend.at[3], wrecv.at[3], {'inner': left}),
          _remote(w1_ref, w1f.at[i], wsend.at[4], wrecv.at[4], {'inner': left})]
    rs[0].start()
    ls[0].start()
    rs[1].start()
    ls[1].start()

    for k in range(md):
        m = s * md + k

        @pl.when(s == 0)
        def _():
            pltpu.make_async_copy(x_ref.at[k], hbuf.at[m], hrecv.at[m]).start()

        @pl.when(s != 0)
        def _():
            _remote(x_ref.at[k], hbuf.at[m], xsend.at[k], hrecv.at[m], {'stage': 0}).start()

    for k in range(md):
        m = s * md + k

        @pl.when(s == ns - 1)
        def _():
            pltpu.make_async_copy(g_ref.at[k], gbuf.at[m], grecv.at[m]).start()

        @pl.when(s != ns - 1)
        def _():
            _remote(g_ref.at[k], gbuf.at[m], xsend.at[md + k], grecv.at[m], {'stage': ns - 1}).start()

    def turn(k):
        w1t[k] = w1f[k].T
        w2t[k] = w2f[k].T

    own1.wait()
    own2.wait()
    turn(i)
    pltpu.make_async_copy(w1f.at[left], w1f.at[left], wrecv.at[0]).wait()
    fr = _remote(w1f.at[left], w1f.at[left], wsend.at[2], wrecv.at[2], {'inner': right})
    fr.start()
    pltpu.make_async_copy(w2f.at[right], w2f.at[right], wrecv.at[3]).wait()
    fl = _remote(w2f.at[right], w2f.at[right], wsend.at[5], wrecv.at[5], {'inner': left})
    fl.start()
    pltpu.make_async_copy(w2f.at[left], w2f.at[left], wrecv.at[1]).wait()
    turn(left)
    pltpu.make_async_copy(w1f.at[right], w1f.at[right], wrecv.at[4]).wait()
    turn(right)
    pltpu.make_async_copy(w1f.at[opp], w1f.at[opp], wrecv.at[2]).wait()
    pltpu.make_async_copy(w2f.at[opp], w2f.at[opp], wrecv.at[5]).wait()

    @pl.when(s >= 2)
    def _():
        turn(opp)

    nc = 256

    def fwd_in(m):
        slot = lax.rem(m, 2)
        pltpu.make_async_copy(hbuf.at[m], hbuf.at[m], hrecv.at[m]).wait()

        @pl.when(m >= 2)
        def _():
            pltpu.make_async_copy(abuf.at[slot], a_ref.at[:, m - 2], asem.at[slot]).wait()
            pltpu.make_async_copy(htb.at[slot], htb.at[slot], htsem.at[slot]).wait()

    def fwd_math(m):
        slot = lax.rem(m, 2)
        h = hbuf[m]
        htb[slot] = h.T
        accs = [None] * (d // nc)

        def down(q):
            for c in range(d // nc):
                r = _dot(abuf[slot, q], w2f[q, :, c * nc:(c + 1) * nc])
                accs[c] = r if q == 0 else accs[c] + r

        for q in range(ni):
            for c in range(f // nc):
                cs = slice(c * nc, (c + 1) * nc)
                u = _dot(h, w1f[q, :, cs])
                p = _gate(u)
                abuf[slot, q, :, cs] = (u * p).astype(BF16)
                gp[m, q, :, cs] = _slope(u, p) if q < ni // 2 else u
            if q > 0:
                down(q - 1)
            yield
        down(ni - 1)
        for c in range(d // nc):
            cs = slice(c * nc, (c + 1) * nc)
            hbuf[m, :, cs] = (h[:, cs].astype(F32) + accs[c]).astype(BF16)

    def fwd_out(m):
        slot = lax.rem(m, 2)
        col = pl.ds(pl.multiple_of(m * b, b), b)
        home = m // md
        kk = lax.rem(m, md)

        @pl.when(s < ns - 1)
        def _():
            _remote(hbuf.at[m], hbuf.at[m], hsend, hrecv.at[m], {'stage': lax.rem(s + 1, ns)}).start()

        @pl.when((s == ns - 1) & ((home == ns - 2) | (home < 2)))
        def _():
            _remote(hbuf.at[m], y_ref.at[kk], hsend, yrecv.at[kk], {'stage': home}).start()

        @pl.when((s == ns - 1) & (home == ns - 1))
        def _():
            pltpu.make_async_copy(hbuf.at[m], y_ref.at[kk], hsend).start()

        pltpu.make_async_copy(abuf.at[slot], a_ref.at[:, m], asem.at[slot]).start()
        pltpu.make_async_copy(htb.at[slot], hg_ref.at[0, :, col], htsem.at[slot]).start()

    def bwd_in(m):
        slot = lax.rem(m, 2)
        pltpu.make_async_copy(gbuf.at[m], gbuf.at[m], grecv.at[m]).wait()

        @pl.when((s == ns - 3) & (m == n - 1))
        def _():
            pl.semaphore_signal(ygo, inc=1, device_id={'stage': ns - 1}, device_id_type=MESH)

        @pl.when(m >= 2)
        def _():
            pltpu.make_async_copy(dubuf.at[slot], du_ref.at[:, m - 2], dusem.at[slot]).wait()
            pltpu.make_async_copy(gtb.at[slot], gtb.at[slot], gtsem.at[slot]).wait()

    def bwd_math(m):
        slot = lax.rem(m, 2)
        g = gbuf[m]
        gtb[slot] = g.T
        accs = [None] * (d // nc)

        def down(q):
            for c in range(d // nc):
                r = _dot(dubuf[slot, q], w1t[q, :, c * nc:(c + 1) * nc])
                accs[c] = r if q == 0 else accs[c] + r

        for q in range(ni):
            for c in range(f // nc):
                cs = slice(c * nc, (c + 1) * nc)
                e = _dot(g, w2t[q, :, cs])
                v = gp[m, q, :, cs]
                if q >= ni // 2:
                    v = _slope(v, _gate(v))
                dubuf[slot, q, :, cs] = (e * v).astype(BF16)
            if q > 0:
                down(q - 1)
            yield
        down(ni - 1)
        for c in range(d // nc):
            cs = slice(c * nc, (c + 1) * nc)
            gbuf[m, :, cs] = (g[:, cs].astype(F32) + accs[c]).astype(BF16)

    def bwd_out(m):
        slot = lax.rem(m, 2)
        col = pl.ds(pl.multiple_of(m * b, b), b)
        home = m // md
        kk = lax.rem(m, md)

        @pl.when(s > 0)
        def _():
            _remote(gbuf.at[m], gbuf.at[m], gsend, grecv.at[m], {'stage': lax.rem(s + ns - 1, ns)}).start()

        @pl.when((s == 0) & (home != 0))
        def _():
            _remote(gbuf.at[m], dx_ref.at[kk], gsend, dxrecv.at[kk], {'stage': home}).start()

        @pl.when((s == 0) & (home == 0))
        def _():
            pltpu.make_async_copy(gbuf.at[m], dx_ref.at[kk], gsend).start()

        pltpu.make_async_copy(dubuf.at[slot], du_ref.at[:, m], dusem.at[slot]).start()
        pltpu.make_async_copy(gtb.at[slot], hg_ref.at[1, :, col], gtsem.at[slot]).start()

    def run(*maths):
        maths = list(maths)
        while maths:
            for g in list(maths):
                if next(g, maths) is maths:
                    maths.remove(g)

    warm = jnp.minimum(1 + 5 * (ns - 1 - s), n)

    def step(t, c):
        mb = t - warm

        @pl.when((t < n) & (t < warm))
        def _():
            fwd_in(t)
            run(fwd_math(t))
            fwd_out(t)

        @pl.when((t < n) & (t >= warm))
        def _():
            fwd_in(t)
            bwd_in(mb)
            run(fwd_math(t), bwd_math(mb))
            fwd_out(t)
            bwd_out(mb)

        @pl.when((t == warm) & (s < 2))
        def _():
            turn(opp)

        @pl.when((t >= n) & (t < warm + n))
        def _():
            bwd_in(mb)
            run(bwd_math(mb))
            bwd_out(mb)

        return c

    lax.fori_loop(0, 2 * n, step, 0)

    @pl.when(s == ns - 1)
    def _():
        pl.semaphore_wait(ygo, 1)
        for home in range(ns - 3, 1, -1):
            for k in range(md):
                _remote(hbuf.at[home * md + k], y_ref.at[k], hsend, yrecv.at[k], {'stage': home}).start()

    for k in range(2):
        pltpu.make_async_copy(abuf.at[k], a_ref.at[:, n - 2 + k], asem.at[k]).wait()
        pltpu.make_async_copy(dubuf.at[k], du_ref.at[:, n - 2 + k], dusem.at[k]).wait()
        pltpu.make_async_copy(htb.at[k], htb.at[k], htsem.at[k]).wait()
        pltpu.make_async_copy(gtb.at[k], gtb.at[k], gtsem.at[k]).wait()
    pltpu.make_async_copy(hbuf, hbuf, hsend).wait()
    pltpu.make_async_copy(gbuf, gbuf, gsend).wait()
    for r in rs + ls + [fr, fl]:
        r.wait_send()
    for k in range(md):
        @pl.when(s != 0)
        def _():
            pltpu.make_async_copy(x_ref.at[k], x_ref.at[k], xsend.at[k]).wait()
            pltpu.make_async_copy(dx_ref.at[k], dx_ref.at[k], dxrecv.at[k]).wait()

        @pl.when(s != ns - 1)
        def _():
            pltpu.make_async_copy(g_ref.at[k], g_ref.at[k], xsend.at[md + k]).wait()
            pltpu.make_async_copy(y_ref.at[k], y_ref.at[k], yrecv.at[k]).wait()


def _wgrad_kernel(ni, nr, hg_ref, a_ref, du_ref, o1_ref, o2_ref,
                  hv, gv, dv, av, s1, s2, r1, r2,
                  lsem, dsem, snd1, snd2, rcv1, rcv2):
    i = lax.axis_index('inner')
    right = lax.rem(i + 1, ni)
    left = lax.rem(i + ni - 1, ni)
    barrier = pltpu.get_barrier_semaphore()
    for nb in (left, right):
        pl.semaphore_signal(barrier, inc=1, device_id={'inner': nb}, device_id_type=MESH)
    def loads(t):
        c1 = lax.rem(i + 2 * ni - 1 - t, ni)
        c2 = lax.rem(i + 1 + t, ni)
        return (pltpu.make_async_copy(du_ref.at[c1], dv.at[t % 2], dsem.at[0, t % 2]),
                pltpu.make_async_copy(a_ref.at[c2], av.at[t % 2], dsem.at[1, t % 2]))

    rows = s1.shape[1]
    k = dv.shape[1] * dv.shape[2]

    def row_loads(r):
        row = pl.ds(pl.multiple_of(r * rows, rows), rows)
        return (pltpu.make_async_copy(hg_ref.at[0, row], hv.at[row], lsem.at[0, r]),
                pltpu.make_async_copy(hg_ref.at[1, row], gv.at[row], lsem.at[1, r]))

    cps = loads(0)
    first = row_loads(0)
    first[0].start()
    cps[0].start()
    first[1].start()
    cps[1].start()
    pl.semaphore_wait(barrier, 2)
    for t in range(ni):
        nxt = loads(t + 1) if t + 1 < ni else None
        slot = t % 2

        def block(r, c):
            row = pl.ds(pl.multiple_of(r * rows, rows), rows)
            if nxt is not None:
                @pl.when(r == 1)
                def _():
                    nxt[0].start()
                    nxt[1].start()
            if t == 0:
                @pl.when(r < nr - 1)
                def _():
                    for cp in row_loads(r + 1):
                        cp.start()
                row_loads(r)[0].wait()

            @pl.when(r == 0)
            def _():
                cps[0].wait()
            p1 = _dot(hv[row, :], dv[slot].reshape(k, dv.shape[3]))
            if t == 0:
                src1 = s1.at[r]
                s1[r] = p1
            else:
                src1 = r1.at[t - 1, r]
                pltpu.make_async_copy(src1, src1, rcv1.at[t - 1, r]).wait()
                if t < ni - 1:
                    r1[t - 1, r] = r1[t - 1, r] + p1
                else:
                    o1_ref[row, :] = r1[t - 1, r] + p1
            if t < ni - 1:
                _remote(src1, r1.at[t, r], snd1, rcv1.at[t, r], {'inner': right}).start()
            if t == 0:
                row_loads(r)[1].wait()

            @pl.when(r == 0)
            def _():
                cps[1].wait()
            p2 = _dot(gv[row, :], av[slot].reshape(k, av.shape[3]))
            if t == 0:
                src2 = s2.at[r]
                s2[r] = p2
            else:
                src2 = r2.at[t - 1, r]
                pltpu.make_async_copy(src2, src2, rcv2.at[t - 1, r]).wait()
                if t < ni - 1:
                    r2[t - 1, r] = r2[t - 1, r] + p2
                else:
                    o2_ref[:, row] = (r2[t - 1, r] + p2).T
            if t < ni - 1:
                _remote(src2, r2.at[t, r], snd2, rcv2.at[t, r], {'inner': left}).start()
            return c

        lax.fori_loop(0, nr, block, 0)
        cps = nxt
    for sem in (snd1, snd2):
        pltpu.make_async_copy(r1, r1, sem).wait()


def _out_kernel(y_ref, dx_ref, w1_ref, w2_ref, yo_ref, dxo_ref, o1_ref, o2_ref, sem):
    cps = [pltpu.make_async_copy(a, o, sem.at[k]) for k, (a, o) in
           enumerate(((w1_ref, o1_ref), (w2_ref, o2_ref), (y_ref, yo_ref), (dx_ref, dxo_ref)))]
    for cp in cps:
        cp.start()
    for cp in cps:
        cp.wait()


def solution(mesh):
    ns = mesh.shape['stage']
    ni = mesh.shape['inner']
    act = P(('data', 'stage', 'inner'), None, None)
    s1 = P(None, 'stage', None, None, 'inner')
    s2 = P(None, 'stage', None, 'inner', None)
    o1 = P('data', 'stage', None, None, 'inner')
    o2 = P('data', 'stage', None, 'inner', None)
    any_ = pl.BlockSpec(memory_space=pl.ANY)
    vmem = pl.BlockSpec(memory_space=pltpu.VMEM)
    dma = pltpu.SemaphoreType.DMA

    def body(x, g, w1, w2):
        md, b, d = x.shape
        f = w1.shape[-1]
        n = ns * md
        sds = jax.ShapeDtypeStruct
        y, dx, hg, a, du = pl.pallas_call(
            functools.partial(_pipe_kernel, ns, ni, md),
            out_shape=(sds((md, b, d), BF16), sds((md, b, d), BF16), sds((2, d, n * b), BF16),
                       sds((ni, n, b, f), BF16), sds((ni, n, b, f), BF16)),
            in_specs=[any_] * 4,
            out_specs=(any_,) * 5,
            scratch_shapes=[
                pltpu.VMEM((ni, d, f), BF16), pltpu.VMEM((ni, f, d), BF16),
                pltpu.VMEM((ni, f, d), BF16), pltpu.VMEM((ni, d, f), BF16),
                pltpu.VMEM((n, b, d), BF16), pltpu.VMEM((n, b, d), BF16),
                pltpu.VMEM((n, ni, b, f), F32),
                pltpu.VMEM((2, d, b), BF16), pltpu.VMEM((2, d, b), BF16),
                pltpu.VMEM((2, ni, b, f), BF16), pltpu.VMEM((2, ni, b, f), BF16),
                dma((6,)), dma((6,)), dma((2,)), dma((2 * md,)), dma((n,)), dma((n,)),
                dma(()), dma(()), dma((md,)), dma((md,)),
                dma((2,)), dma((2,)), dma((2,)), dma((2,)), pltpu.SemaphoreType.REGULAR,
            ],
            compiler_params=pltpu.CompilerParams(collective_id=0, has_side_effects=True, vmem_limit_bytes=63 * 2**20),
            name='pipe',
        )(x, g, w1[0, 0, 0], w2[0, 0, 0])
        nr = d // b
        dw1, dw2 = pl.pallas_call(
            functools.partial(_wgrad_kernel, ni, nr),
            out_shape=(sds((d, f), F32), sds((f, d), F32)),
            in_specs=[any_] * 3,
            out_specs=(vmem, vmem),
            scratch_shapes=[
                pltpu.VMEM((d, n * b), BF16), pltpu.VMEM((d, n * b), BF16),
                pltpu.VMEM((2, n, b, f), BF16), pltpu.VMEM((2, n, b, f), BF16),
                pltpu.VMEM((nr, b, f), F32), pltpu.VMEM((nr, b, f), F32),
                pltpu.VMEM((ni - 1, nr, b, f), F32), pltpu.VMEM((ni - 1, nr, b, f), F32),
                dma((2, nr)), dma((2, 2)), dma(()), dma(()),
                dma((ni - 1, nr)), dma((ni - 1, nr)),
            ],
            compiler_params=pltpu.CompilerParams(collective_id=1, has_side_effects=True, vmem_limit_bytes=48 * 2**20),
            name='wgrad',
        )(hg, a, du)
        y, dx, dw1, dw2 = pl.pallas_call(
            _out_kernel,
            out_shape=(sds(y.shape, BF16), sds(dx.shape, BF16), sds(dw1.shape, F32), sds(dw2.shape, F32)),
            in_specs=[vmem] * 4,
            out_specs=(any_,) * 4,
            scratch_shapes=[dma((4,))],
            compiler_params=pltpu.CompilerParams(vmem_limit_bytes=2**20),
            name='out',
        )(y, dx, dw1, dw2)
        return y, dx, dw1[None, None, None], dw2[None, None, None]

    return jax.shard_map(body, mesh=mesh, in_specs=(act, act, s1, s2), out_specs=(act, act, o1, o2), check_vma=False)
```

time: 406 us -> 355 us (0.87)
  Pallas kernels: 399 us -> 354 us
  local copies, waits for them, and re-layouts: 6.28 us -> 0.01 us
    pallas_call x1, Pallas kernels: 243 us -> 197 us  [body(): pl.pallas_call(functools.partial(_pipe_kernel, ns, ni, md), out_shape=(sd...]
    unnamed x10 -> x4, local copies, waits for them, and re-layouts: 6.28 us -> 0.01 us
where the time goes in v2:
time: 355 us
  Pallas kernels  354 us (100%)
    pallas_call x1, Pallas kernels, body(): pl.pallas_call(functools.partial(_pipe_kernel, ns, ni, md), out_shape=(sd...  197 us
    pallas_call x1, Pallas kernels, body(): pl.pallas_call(functools.partial(_wgrad_kernel, ni, nr), out_shape=(sds((...  154 us

profile of v2, /device:TPU:103, one launch (start us, length us, event | category | flops | bytes accessed | tf_op | source)
XLA Modules:
  0.0 354.9 jit_solution(13067727396818622266)
XLA Ops:
  0.6 197.2 %pipe.1 = (bf16[2,128,768]{2,1,0:T(8,128)(2,1)}, bf16[2,128,768]{2,1,0:T(8,128)(2,1)}, bf16[2,768,2048]{2,1,0:T(8,128)(2,1)}, bf16[4,16,128,768]{3,2,1,0:T(8,128)(2,1)}, bf16[4,16,128,768]{3,2,1,0:T(8,128)(2,1)}) custom-call(bf16[2,128,768]{2,1,0:T(8,128)(2,1)} %x_ref.1, bf16[2,128,768]{2,1,0:T(8,128)(2,1)} %g_ref.1, bf16[768,768]{1,0:T(8,128)(2,1)} %bitcast.4, ...), custom_call_target="tpu_custom_call" | custom-call | tf_op jit(solution)/shard_map/pipe/pallas_call | solution.py:422
  197.9 0.0 copy-start
  197.9 0.0 copy-start.1
  197.9 154.4 %wgrad.1 = (f32[768,768]{1,0:T(8,128)S(1)}, f32[768,768]{1,0:T(8,128)S(1)}) custom-call(bf16[2,768,2048]{2,1,0:T(8,128)(2,1)} %get-tuple-element.17.hg_ref, bf16[4,16,128,768]{3,2,1,0:T(8,128)(2,1)} %get-tuple-element.18.a_ref, bf16[4,16,128,768]{3,2,1,0:T(8,128)(2,1)} %get-tuple-element.19.du_ref), custom_call_target="tpu_custom_call" | custom-call | tf_op jit(solution)/shard_map/wgrad/pallas_call | solution.py:443
  352.3 0.0 copy-done
  352.3 0.0 copy-done.1
  352.3 2.5 out.1
Async XLA Ops:
  197.9 154.4 %copy-start = (bf16[2,128,768]{2,1,0:T(8,128)(2,1)S(1)}, bf16[2,128,768]{2,1,0:T(8,128)(2,1)}, u32[]{:S(2)}) copy-start(bf16[2,128,768]{2,1,0:T(8,128)(2,1)} %get-tuple-element.15.y_ref) | copy-start | bytes 1179652
  197.9 154.4 %copy-start.1 = (bf16[2,128,768]{2,1,0:T(8,128)(2,1)S(1)}, bf16[2,128,768]{2,1,0:T(8,128)(2,1)}, u32[]{:S(2)}) copy-start(bf16[2,128,768]{2,1,0:T(8,128)(2,1)} %get-tuple-element.16.dx_ref) | copy-start | bytes 1179652

commit v3 on v2

--- a/solution.py
+++ b/solution.py
@@ -38,7 +38,7 @@
                  y_ref, dx_ref, hg_ref, a_ref, du_ref,
                  w1f, w2f, w1t, w2t, hbuf, gbuf, gp, htb, gtb, abuf, dubuf,
                  wsend, wrecv, wloc, xsend, hrecv, grecv, hsend, gsend, yrecv, dxrecv,
-                 htsem, gtsem, asem, dusem, ygo):
+                 htsem, gtsem, asem, dusem, ygo, wgo):
     s = lax.axis_index('stage')
     i = lax.axis_index('inner')
     n = ns * md
@@ -60,17 +60,29 @@
     own2.start()
     pl.semaphore_wait(barrier, ns + 1)
 
-    rs = [_remote(w1_ref, w1f.at[i], wsend.at[0], wrecv.at[0], {'inner': right}),
+    e = d // 4
+    lead = [_remote(w1_ref.at[:e], w1f.at[i, :e], wsend.at[6], wrecv.at[0], {'inner': right}),
+            _remote(w2_ref.at[:e], w2f.at[i, :e], wsend.at[7], wrecv.at[3], {'inner': left})]
+    rs = [_remote(w1_ref.at[e:], w1f.at[i, e:], wsend.at[0], wrecv.at[0], {'inner': right}),
           _remote(w2_ref, w2f.at[i], wsend.at[1], wrecv.at[1], {'inner': right})]
-    ls = [_remote(w2_ref, w2f.at[i], wsend.at[3], wrecv.at[3], {'inner': left}),
+    ls = [_remote(w2_ref.at[e:], w2f.at[i, e:], wsend.at[3], wrecv.at[3], {'inner': left}),
           _remote(w1_ref, w1f.at[i], wsend.at[4], wrecv.at[4], {'inner': left})]
-    rs[0].start()
-    ls[0].start()
-    rs[1].start()
-    ls[1].start()
+
+    @pl.when(lax.rem(s, 2) == 1)
+    def _():
+        pl.semaphore_wait(wgo, 1)
+
+    for r in (lead[0], lead[1], rs[0], ls[0], rs[1], ls[1]):
+        r.start()
+    for r in lead:
+        r.wait_send()
+
+    @pl.when(lax.rem(s, 2) == 0)
+    def _():
+        pl.semaphore_signal(wgo, inc=1, device_id={'stage': s + 1}, device_id_type=MESH)
 
     for k in range(md):
-        m = s * md + k
+        m = lax.rem(s + ns - 1, ns) * md + k
 
         @pl.when(s == 0)
         def _():
@@ -81,7 +93,7 @@
             _remote(x_ref.at[k], hbuf.at[m], xsend.at[k], hrecv.at[m], {'stage': 0}).start()
 
     for k in range(md):
-        m = s * md + k
+        m = lax.rem(s + ns - 1, ns) * md + k
 
         @pl.when(s == ns - 1)
         def _():
@@ -155,7 +167,7 @@
     def fwd_out(m):
         slot = lax.rem(m, 2)
         col = pl.ds(pl.multiple_of(m * b, b), b)
-        home = m // md
+        home = lax.rem(m // md + 1, ns)
         kk = lax.rem(m, md)
 
         @pl.when(s < ns - 1)
@@ -216,7 +228,7 @@
     def bwd_out(m):
         slot = lax.rem(m, 2)
         col = pl.ds(pl.multiple_of(m * b, b), b)
-        home = m // md
+        home = lax.rem(m // md + 1, ns)
         kk = lax.rem(m, md)
 
         @pl.when(s > 0)
@@ -257,8 +269,8 @@
             fwd_in(t)
             bwd_in(mb)
             run(fwd_math(t), bwd_math(mb))
+            bwd_out(mb)
             fwd_out(t)
-            bwd_out(mb)
 
         @pl.when((t == warm) & (s < 2))
         def _():
@@ -279,7 +291,7 @@
         pl.semaphore_wait(ygo, 1)
         for home in range(ns - 3, 1, -1):
             for k in range(md):
-                _remote(hbuf.at[home * md + k], y_ref.at[k], hsend, yrecv.at[k], {'stage': home}).start()
+                _remote(hbuf.at[(home - 1) * md + k], y_ref.at[k], hsend, yrecv.at[k], {'stage': home}).start()
 
     for k in range(2):
         pltpu.make_async_copy(abuf.at[k], a_ref.at[:, n - 2 + k], asem.at[k]).wait()
@@ -432,9 +444,9 @@
                 pltpu.VMEM((n, ni, b, f), F32),
                 pltpu.VMEM((2, d, b), BF16), pltpu.VMEM((2, d, b), BF16),
                 pltpu.VMEM((2, ni, b, f), BF16), pltpu.VMEM((2, ni, b, f), BF16),
-                dma((6,)), dma((6,)), dma((2,)), dma((2 * md,)), dma((n,)), dma((n,)),
+                dma((8,)), dma((6,)), dma((2,)), dma((2 * md,)), dma((n,)), dma((n,)),
                 dma(()), dma(()), dma((md,)), dma((md,)),
-                dma((2,)), dma((2,)), dma((2,)), dma((2,)), pltpu.SemaphoreType.REGULAR,
+                dma((2,)), dma((2,)), dma((2,)), dma((2,)), pltpu.SemaphoreType.REGULAR, pltpu.SemaphoreType.REGULAR,
             ],
             compiler_params=pltpu.CompilerParams(collective_id=0, has_side_effects=True, vmem_limit_bytes=63 * 2**20),
             name='pipe',

time: 355 us -> 350 us (0.986)
  Pallas kernels: 354 us -> 347 us
    pallas_call x1, Pallas kernels: 197 us -> 190 us  [body(): pl.pallas_call(functools.partial(_pipe_kernel, ns, ni, md), out_shape=(sd...]
where the time goes in v3:
time: 350 us; the launch traced here: 348 us
  Pallas kernels  347 us (99%)
    pallas_call x1, Pallas kernels, body(): pl.pallas_call(functools.partial(_pipe_kernel, ns, ni, md), out_shape=(sd...  190 us
    pallas_call x1, Pallas kernels, body(): pl.pallas_call(functools.partial(_wgrad_kernel, ni, nr), out_shape=(sds((...  154 us

profile of v3, /device:TPU:103, one launch (start us, length us, event | category | flops | bytes accessed | tf_op | source)
XLA Modules:
  0.0 347.9 jit_solution(10177017200650923885)
XLA Ops:
  0.6 190.2 %pipe.1 = (bf16[2,128,768]{2,1,0:T(8,128)(2,1)}, bf16[2,128,768]{2,1,0:T(8,128)(2,1)}, bf16[2,768,2048]{2,1,0:T(8,128)(2,1)}, bf16[4,16,128,768]{3,2,1,0:T(8,128)(2,1)}, bf16[4,16,128,768]{3,2,1,0:T(8,128)(2,1)}) custom-call(bf16[2,128,768]{2,1,0:T(8,128)(2,1)} %x_ref.1, bf16[2,128,768]{2,1,0:T(8,128)(2,1)} %g_ref.1, bf16[768,768]{1,0:T(8,128)(2,1)} %bitcast.4, ...), custom_call_target="tpu_custom_call" | custom-call | tf_op jit(solution)/shard_map/pipe/pallas_call | solution.py:434
  190.9 0.0 copy-start
  190.9 0.0 copy-start.1
  190.9 154.4 %wgrad.1 = (f32[768,768]{1,0:T(8,128)S(1)}, f32[768,768]{1,0:T(8,128)S(1)}) custom-call(bf16[2,768,2048]{2,1,0:T(8,128)(2,1)} %get-tuple-element.17.hg_ref, bf16[4,16,128,768]{3,2,1,0:T(8,128)(2,1)} %get-tuple-element.18.a_ref, bf16[4,16,128,768]{3,2,1,0:T(8,128)(2,1)} %get-tuple-element.19.du_ref), custom_call_target="tpu_custom_call" | custom-call | tf_op jit(solution)/shard_map/wgrad/pallas_call | solution.py:455
  345.3 0.0 copy-done
  345.3 0.0 copy-done.1
  345.3 2.5 out.1
Async XLA Ops:
  190.9 154.4 %copy-start = (bf16[2,128,768]{2,1,0:T(8,128)(2,1)S(1)}, bf16[2,128,768]{2,1,0:T(8,128)(2,1)}, u32[]{:S(2)}) copy-start(bf16[2,128,768]{2,1,0:T(8,128)(2,1)} %get-tuple-element.15.y_ref) | copy-start | bytes 1179652
  190.9 154.4 %copy-start.1 = (bf16[2,128,768]{2,1,0:T(8,128)(2,1)S(1)}, bf16[2,128,768]{2,1,0:T(8,128)(2,1)}, u32[]{:S(2)}) copy-start(bf16[2,128,768]{2,1,0:T(8,128)(2,1)} %get-tuple-element.16.dx_ref) | copy-start | bytes 1179652

commit v4 on v3

--- a/solution.py
+++ b/solution.py
@@ -365,7 +365,11 @@
             @pl.when(r == 0)
             def _():
                 cps[0].wait()
+                if t > 0:
+                    cps[1].wait()
             p1 = _dot(hv[row, :], dv[slot].reshape(k, dv.shape[3]))
+            if t > 0:
+                p2 = _dot(gv[row, :], av[slot].reshape(k, av.shape[3]))
             if t == 0:
                 src1 = s1.at[r]
                 s1[r] = p1
@@ -381,11 +385,11 @@
             if t == 0:
                 row_loads(r)[1].wait()
 
-            @pl.when(r == 0)
-            def _():
-                cps[1].wait()
-            p2 = _dot(gv[row, :], av[slot].reshape(k, av.shape[3]))
+                @pl.when(r == 0)
+                def _():
+                    cps[1].wait()
             if t == 0:
+                p2 = _dot(gv[row, :], av[slot].reshape(k, av.shape[3]))
                 src2 = s2.at[r]
                 s2[r] = p2
             else:

time: 350 us -> 349 us (level)
  no operation moved by 1% of the time
where the time goes in v4:
time: 349 us; the launch traced here: 347 us
  Pallas kernels  346 us (99%)
    pallas_call x1, Pallas kernels, body(): pl.pallas_call(functools.partial(_pipe_kernel, ns, ni, md), out_shape=(sd...  190 us
    pallas_call x1, Pallas kernels, body(): pl.pallas_call(functools.partial(_wgrad_kernel, ni, nr), out_shape=(sds((...  154 us

profile of v4, /device:TPU:103, one launch (start us, length us, event | category | flops | bytes accessed | tf_op | source)
XLA Modules:
  0.0 347.2 jit_solution(5337623877101730683)
XLA Ops:
  0.6 190.2 %pipe.1 = (bf16[2,128,768]{2,1,0:T(8,128)(2,1)}, bf16[2,128,768]{2,1,0:T(8,128)(2,1)}, bf16[2,768,2048]{2,1,0:T(8,128)(2,1)}, bf16[4,16,128,768]{3,2,1,0:T(8,128)(2,1)}, bf16[4,16,128,768]{3,2,1,0:T(8,128)(2,1)}) custom-call(bf16[2,128,768]{2,1,0:T(8,128)(2,1)} %x_ref.1, bf16[2,128,768]{2,1,0:T(8,128)(2,1)} %g_ref.1, bf16[768,768]{1,0:T(8,128)(2,1)} %bitcast.4, ...), custom_call_target="tpu_custom_call" | custom-call | tf_op jit(solution)/shard_map/pipe/pallas_call | solution.py:438
  190.9 0.0 copy-start
  190.9 0.0 copy-start.1
  190.9 153.7 %wgrad.1 = (f32[768,768]{1,0:T(8,128)S(1)}, f32[768,768]{1,0:T(8,128)S(1)}) custom-call(bf16[2,768,2048]{2,1,0:T(8,128)(2,1)} %get-tuple-element.17.hg_ref, bf16[4,16,128,768]{3,2,1,0:T(8,128)(2,1)} %get-tuple-element.18.a_ref, bf16[4,16,128,768]{3,2,1,0:T(8,128)(2,1)} %get-tuple-element.19.du_ref), custom_call_target="tpu_custom_call" | custom-call | tf_op jit(solution)/shard_map/wgrad/pallas_call | solution.py:459
  344.6 0.0 copy-done
  344.6 0.0 copy-done.1
  344.6 2.5 out.1
Async XLA Ops:
  190.9 153.7 %copy-start = (bf16[2,128,768]{2,1,0:T(8,128)(2,1)S(1)}, bf16[2,128,768]{2,1,0:T(8,128)(2,1)}, u32[]{:S(2)}) copy-start(bf16[2,128,768]{2,1,0:T(8,128)(2,1)} %get-tuple-element.15.y_ref) | copy-start | bytes 1179652
  190.9 153.7 %copy-start.1 = (bf16[2,128,768]{2,1,0:T(8,128)(2,1)S(1)}, bf16[2,128,768]{2,1,0:T(8,128)(2,1)}, u32[]{:S(2)}) copy-start(bf16[2,128,768]{2,1,0:T(8,128)(2,1)} %get-tuple-element.16.dx_ref) | copy-start | bytes 1179652
